TPU v7x, 32 devices: a whole 2x2x4 slice. The times are simulated.
32 devices in a mesh: row: 4 (over z), col: 8 (over y, x, core).
Axes of the slice: x: 2, y: 2, z: 4, core: 2. Of those that a mesh axis runs over, the one named last changes fastest.
Arguments:
- factor: bfloat16 [32768, 5, 1024], P('col', None, 'row'), may hold values from -0.0625 to 0.0625
- diag_inverse: bfloat16 [5, 1024, 1024], P(None, 'row'), may hold values from -1 to 2
- right_side: float32 [16, 32, 1024], P(None, 'col', 'row'), may hold values from -6 to 6
- tile_order: int32 [32], replicated, may hold values from 0 to 31, each once
- live_segments: int32 [16], replicated, may hold values from 2 to 5
Outputs:
- result: float32 [16, 32, 1024], P(None, 'col', 'row')
Inputs may be any that keep to these rules, and one draw needn't show every extreme that they name: `tile_order`: each of 0 to 31 appears once.
All inputs are finite; a program needn't handle non-finite values.
Results may differ from a plain program's by a relative error of at most 0.0019.
Values may be sent and summed in bfloat16 or wider, within the bound.
A program may use at most 64 MiB of HBM per device.

v0:
```python
import jax
import jax.numpy as jnp
from jax import lax
from jax.sharding import PartitionSpec as P


def spread(block, axis, owner):
    block = jnp.where(lax.axis_index(axis) == owner, block, jnp.zeros_like(block))
    return lax.psum(block, axis)


def per_device(factor, diag_inverse, right_side, tile_order, live_segments):
    section_count = diag_inverse.shape[0]
    slice_width = diag_inverse.shape[1]
    tile_width = diag_inverse.shape[2]
    rhs_count = right_side.shape[0]
    rows_dev = right_side.shape[1]
    my_col = lax.axis_index("col")
    my_row = lax.axis_index("row")
    slice_start = my_row * slice_width
    partial_value = jnp.zeros((rhs_count, rows_dev * tile_width), jnp.float32)
    result = jnp.zeros((rhs_count, rows_dev, slice_width), jnp.float32)
    for section in range(section_count):
        slot_id = tile_order[section]
        root_col = slot_id // rows_dev
        local_pos = slot_id % rows_dev
        part_tile = lax.dynamic_slice_in_dim(partial_value, local_pos * tile_width, tile_width, 1)
        rhs_slice = lax.dynamic_index_in_dim(right_side, local_pos, 1, keepdims=False)
        placed = lax.dynamic_update_slice_in_dim(
            jnp.zeros((rhs_count, tile_width), jnp.float32), rhs_slice, slice_start, 1
        )
        remaining = lax.psum(placed - part_tile, "row")
        inverse = diag_inverse[section].astype(jnp.float32)
        solved = lax.dot_general(
            remaining,
            inverse,
            (((1,), (1,)), ((), ())),
            precision=lax.Precision.HIGHEST,
            preferred_element_type=jnp.float32,
        )
        is_live = (section < live_segments)[:, None]
        sent_block = jnp.where(is_live, solved, jnp.zeros_like(solved)).astype(jnp.bfloat16)
        sent_block = spread(sent_block, "col", root_col)
        kept_part = lax.dynamic_slice_in_dim(remaining, slice_start, slice_width, 1)
        stored = jnp.where(is_live, solved, kept_part)
        written = lax.dynamic_update_slice_in_dim(result, stored[:, None, :], local_pos, 1)
        result = jnp.where(my_col == root_col, written, result)
        panel_rows = factor[:, section, :]
        partial_value = partial_value + lax.dot_general(
            sent_block, panel_rows, (((1,), (1,)), ((), ())), preferred_element_type=jnp.float32
        )
    shaped = partial_value.reshape(rhs_count, rows_dev, tile_width)
    total_part = lax.psum_scatter(shaped, "row", scatter_dimension=2, tiled=True)
    local_slots = my_col * rows_dev + jnp.arange(rows_dev, dtype=jnp.int32)
    visited = jnp.any(local_slots[:, None] == tile_order[:section_count][None, :], axis=1)
    return jnp.where(visited[None, :, None], result, right_side - total_part)


def solution(mesh):
    return jax.shard_map(
        per_device,
        mesh=mesh,
        in_specs=(P("col", None, "row"), P(None, "row", None), P(None, "col", "row"), P(), P()),
        out_specs=P(None, "col", "row"),
        check_vma=False,
    )
```

profile of v0, /device:TPU:0, one launch (start us, length us, event | category | flops | bytes accessed | tf_op | source)
XLA Modules:
  0.0 292.0 jit_solution(3287406973859240953)
XLA Ops:
  6.5 1.5 fusion.35
  10.1 0.9 copy.16
  22.0 26.9 %all-reduce.6.cloned.1.call-done = f32[16,1024]{1,0:T(8,128)} async-done(((f32[16,1024]{1,0:T(8,128)}), f32[16,1024]{1,0:T(8,128)}) %all-reduce.6.cloned.1.call-update) | async-done | bytes 65552 | tf_op jit(solution)/shard_map/psum | solution.py:32
  48.9 1.6 bitcast_dynamic-update-slice_fusion.4
  50.5 12.1 %psum.71 = bf16[16,256]{1,0:T(8,128)(2,1)S(1)} all-reduce(bf16[16,256]{1,0:T(8,128)(2,1)S(1)} %fusion.30), channel_id=1, replica_groups=mesh['row'=4,'col'=8] {'col'}, use_global_device_ids=true, to_apply=%region_2.3 | all-reduce | flops 4096 | bytes 16384 | tf_op jit(solution)/shard_map/psum | solution.py:9
  62.7 2.2 fusion.4
  65.7 33.1 %all-reduce.8.cloned.1.call-done = f32[16,1024]{1,0:T(8,128)} async-done(((f32[16,1024]{1,0:T(8,128)}), f32[16,1024]{1,0:T(8,128)}) %all-reduce.8.cloned.1.call-update) | async-done | bytes 65552 | tf_op jit(solution)/shard_map/psum | solution.py:32
  98.8 1.4 fusion.29
  100.3 12.1 %psum.73 = bf16[16,256]{1,0:T(8,128)(2,1)S(1)} all-reduce(bf16[16,256]{1,0:T(8,128)(2,1)S(1)} %fusion.31), channel_id=1, replica_groups=mesh['row'=4,'col'=8] {'col'}, use_global_device_ids=true, to_apply=%region_4.5 | all-reduce | flops 4096 | bytes 16384 | tf_op jit(solution)/shard_map/psum | solution.py:9
  112.4 2.2 convolution_add_fusion.3
  115.4 33.1 %all-reduce.10.cloned.1.call-done = f32[16,1024]{1,0:T(8,128)} async-done(((f32[16,1024]{1,0:T(8,128)}), f32[16,1024]{1,0:T(8,128)}) %all-reduce.10.cloned.1.call-update) | async-done | bytes 65552 | tf_op jit(solution)/shard_map/psum | solution.py:32
  148.5 1.4 fusion.28
  150.0 12.1 %psum.75 = bf16[16,256]{1,0:T(8,128)(2,1)S(1)} all-reduce(bf16[16,256]{1,0:T(8,128)(2,1)S(1)} %fusion.32), channel_id=1, replica_groups=mesh['row'=4,'col'=8] {'col'}, use_global_device_ids=true, to_apply=%region_6.7 | all-reduce | flops 4096 | bytes 16384 | tf_op jit(solution)/shard_map/psum | solution.py:9
  162.1 2.2 convolution_add_fusion.2
  165.1 33.1 %all-reduce.12.cloned.1.call-done = f32[16,1024]{1,0:T(8,128)} async-done(((f32[16,1024]{1,0:T(8,128)}), f32[16,1024]{1,0:T(8,128)}) %all-reduce.12.cloned.1.call-update) | async-done | bytes 65552 | tf_op jit(solution)/shard_map/psum | solution.py:32
  198.3 1.4 fusion.27
  199.7 12.1 %psum.77 = bf16[16,256]{1,0:T(8,128)(2,1)S(1)} all-reduce(bf16[16,256]{1,0:T(8,128)(2,1)S(1)} %fusion.33), channel_id=1, replica_groups=mesh['row'=4,'col'=8] {'col'}, use_global_device_ids=true, to_apply=%region_8.9 | all-reduce | flops 4096 | bytes 16384 | tf_op jit(solution)/shard_map/psum | solution.py:9
  211.9 2.2 convolution_add_fusion.1
  215.5 32.5 %all-reduce.14.cloned.1.call-done = f32[16,1024]{1,0:T(8,128)} async-done(((f32[16,1024]{1,0:T(8,128)}), f32[16,1024]{1,0:T(8,128)}) %all-reduce.14.cloned.1.call-update) | async-done | bytes 65552 | tf_op jit(solution)/shard_map/psum | solution.py:32
  248.0 1.4 fusion.26
  249.5 12.1 %psum.79 = bf16[16,256]{1,0:T(8,128)(2,1)S(1)} all-reduce(bf16[16,256]{1,0:T(8,128)(2,1)S(1)} %fusion.34), channel_id=1, replica_groups=mesh['row'=4,'col'=8] {'col'}, use_global_device_ids=true, to_apply=%region_10.11 | all-reduce | flops 4096 | bytes 16384 | tf_op jit(solution)/shard_map/psum | solution.py:9
  261.6 2.2 convolution_add_fusion
  264.8 18.8 %reduce-scatter.2.cloned.1.call-done = f32[16,4,256]{2,0,1:T(8,128)} async-done(((f32[16,4,1024]{2,0,1:T(8,128)}), f32[16,4,256]{2,0,1:T(8,128)}) %reduce-scatter.2.cloned.1.call-update) | async-done | bytes 65552 | tf_op jit(solution)/shard_map/reduce_scatter | solution.py:53
  283.5 0.9 subtract_select_fusion
  (45 shorter events, 6.3 us)
Async XLA Ops:
  6.5 92.3 %copy-start = (bf16[5,256,1024]{2,1,0:T(8,128)(2,1)S(1)}, bf16[5,256,1024]{2,1,0:T(8,128)(2,1)}, u32[]{:S(2)}) copy-start(bf16[5,256,1024]{2,1,0:T(8,128)(2,1)} %param.6) | copy-start | bytes 7864324
  6.5 42.3 %all-reduce.6.cloned.1.call-start = ((), (), s32[]{:S(2)}) async-start(), calls=%async_computation.1 | async-start | bytes 131072 | tf_op jit(solution)/shard_map/psum | solution.py:32
  11.0 0.6 copy-start.1
  11.7 87.1 %all-reduce.8.cloned.1.call-start = ((), (), s32[]{:S(2)}) async-start(), calls=%async_computation.2 | async-start | bytes 131072 | tf_op jit(solution)/shard_map/psum | solution.py:32
  65.6 83.0 %all-reduce.10.cloned.1.call-start = ((), (), s32[]{:S(2)}) async-start(), calls=%async_computation.3 | async-start | bytes 131072 | tf_op jit(solution)/shard_map/psum | solution.py:32
  115.3 83.0 %all-reduce.12.cloned.1.call-start = ((), (), s32[]{:S(2)}) async-start(), calls=%async_computation.4 | async-start | bytes 131072 | tf_op jit(solution)/shard_map/psum | solution.py:32
  165.0 83.0 %all-reduce.14.cloned.1.call-start = ((), (), s32[]{:S(2)}) async-start(), calls=%async_computation.5 | async-start | bytes 131072 | tf_op jit(solution)/shard_map/psum | solution.py:32
  214.1 50.5 %copy-start.3 = (s32[32]{0:T(128)S(1)}, s32[32]{0:T(128)}, u32[]{:S(2)}) copy-start(s32[32]{0:T(128)} %param.8) | copy-start | bytes 388
  214.1 69.4 %copy-start.2 = (f32[16,4,256]{2,1,0:T(4,128)S(1)}, f32[16,4,256]{2,1,0:T(4,128)}, u32[]{:S(2)}) copy-start(f32[16,4,256]{2,1,0:T(4,128)} %param.7) | copy-start | bytes 196612
  214.8 68.8 %reduce-scatter.2.cloned.1.call-start = ((), (), s32[]{:S(2)}) async-start(), calls=%async_computation.6 | async-start | bytes 327680 | tf_op jit(solution)/shard_map/reduce_scatter | solution.py:53
Sparse Core Ops, SparseCore 0:
  11.8 37.0 all-reduce.5
  65.7 33.0 all-reduce.7
  115.4 33.0 all-reduce.9
  165.2 33.0 all-reduce.11
  214.9 33.0 all-reduce.13
  264.7 18.7 reduce-scatter.1
where the time goes:
time: 293 us; the launch traced here: 292 us
  waiting for transfers between devices  178 us (61%)
  blocking collectives  60.6 us (21%)
  between operations  26 us (9%)
  matrix products  18.2 us (6%)
  other arithmetic  4.76 us (2%)
  local copies, waits for them, and re-layouts  4.48 us (2%)
    psum x5, waiting for transfers between devices, per_device(): remaining = lax.psum(placed - part_tile, 'row')  159 us
    psum x5, blocking collectives, spread(): return lax.psum(block, axis)  60.6 us
    reduce_scatter x1, waiting for transfers between devices, per_device(): lax.psum_scatter(shaped, 'row', scatter_dimension=2, tiled=True)  18.8 us
    dot_general x5, matrix products, per_device(): lax.dot_general(sent_block, panel_rows, (((1,), (1,)), ((), ())), preferr...  11.2 us
    dot_general x5, matrix products, per_device(): lax.dot_general(remaining, inverse, (((1,), (1,)), ((), ())), precision=l...  7.03 us
  transfers between devices with their start and end apart: 6, of which 6 were waited for; matrix products, arithmetic and copies ran while one was open for 0% of the time, Pallas kernels for 0%

commit v1 on v0

v1 whole, which is shorter than its diff:
```python
import functools
import jax
import jax.numpy as jnp
from jax import lax
from jax.experimental import pallas as pl
from jax.experimental.pallas import tpu as pltpu
from jax.sharding import PartitionSpec as P

MESH = pl.DeviceIdType.MESH
NT = (((1,), (1,)), ((), ()))


def remote(src, dst, send_sem, recv_sem, axis, peer):
    return pltpu.make_async_remote_copy(
        src_ref=src, dst_ref=dst, send_sem=send_sem, recv_sem=recv_sem,
        device_id={axis: peer}, device_id_type=MESH,
    )


def kernel(
    rows, cols, factor_hbm, inverse_hbm, rhs, order, live, out,
    factor, inverse, first, part_out, part_in, sent_all, stored, acc, tail_out, tail_in,
    factor_sem, inverse_sem, first_sems, part_sems, sent_sems, tail_sems,
):
    sections = len(factor)
    rows_dev, tile, width = factor[0].shape
    rhs_count = rhs.shape[0]
    r, c = lax.axis_index("row"), lax.axis_index("col")

    loads = []
    for u in range(sections):
        pair = (
            pltpu.make_async_copy(inverse_hbm.at[u], inverse.at[u], inverse_sem.at[u]),
            pltpu.make_async_copy(factor_hbm.at[u], factor[u], factor_sem.at[u]),
        )
        for copy in pair:
            copy.start()
        loads.append(pair)

    barrier = pltpu.get_barrier_semaphore()
    for axis, me, count in (("row", r, rows), ("col", c, cols)):
        for d in range(1, count):
            pl.semaphore_signal(
                barrier, inc=1, device_id={axis: lax.rem(me + d, count)}, device_id_type=MESH
            )

    slots = [order[u] for u in range(sections)]
    roots = [lax.div(s, rows_dev) for s in slots]
    locals_ = [lax.rem(s, rows_dev) for s in slots]
    row_ids = lax.broadcasted_iota(jnp.int32, (rhs_count, width), 0)
    limit = jnp.zeros((rhs_count, width), jnp.int32)
    for k in range(rhs_count):
        limit = jnp.where(row_ids == k, live[k], limit)

    def rhs_of(local):
        picked = rhs[:, 0, :]
        for j in range(1, rows_dev):
            picked = jnp.where(local == j, rhs[:, j, :], picked)
        return picked

    for j in range(rows_dev):
        acc[j] = jnp.zeros((rhs_count, tile), jnp.float32)
    first[r] = rhs_of(locals_[0])

    pl.semaphore_wait(barrier, rows - 1 + cols - 1)

    pending = []
    copies = []
    for d in range(1, rows):
        copy = remote(
            first.at[r], first.at[r], first_sems.at[0, d], first_sems.at[1, d],
            "row", lax.rem(r + d, rows),
        )
        copy.start()
        copies.append(copy)
    pending += copies

    own = None
    for t in range(sections):
        for copy in copies:
            copy.wait_recv()
        if t == 0:
            remaining = jnp.concatenate([first[s] for s in range(rows)], axis=1)
            kept = first[r]
        else:
            remaining = own
            for d in range(1, rows):
                remaining = remaining + part_in[t, d]
            kept = remaining[:, :width]
            for s in range(1, rows):
                kept = jnp.where(r == s, remaining[:, s * width:(s + 1) * width], kept)
        high = remaining.astype(jnp.bfloat16)
        rest = remaining - high.astype(jnp.float32)
        middle = rest.astype(jnp.bfloat16)
        low = (rest - middle.astype(jnp.float32)).astype(jnp.bfloat16)
        loads[t][0].wait()
        parts = lax.dot_general(
            jnp.concatenate([high, middle, low], axis=0), inverse[t], NT,
            preferred_element_type=jnp.float32,
        )
        solved = (
            parts[2 * rhs_count:] + parts[rhs_count:2 * rhs_count]
        ) + parts[:rhs_count]
        is_live = limit > t
        sent_all[t][c] = jnp.where(is_live, solved, 0.0).astype(jnp.bfloat16)
        sends = []
        for d in range(1, cols):
            copy = remote(
                sent_all[t].at[c], sent_all[t].at[c], sent_sems.at[0, t, d],
                sent_sems.at[1, t, d], "col", lax.rem(c + d, cols),
            )
            copy.start()
            sends.append(copy)
        pending += sends
        stored[t] = jnp.where(is_live, solved, kept)
        loads[t][1].wait()
        for copy in sends:
            copy.wait_recv()
        sent = sent_all[t][roots[t]]
        if t + 1 < sections:
            local = locals_[t + 1]
            update = acc[local] + lax.dot_general(
                sent, factor[t][local], NT, preferred_element_type=jnp.float32
            )
            mine = rhs_of(local)
            own = jnp.concatenate(
                [jnp.where(r == s, mine, 0.0) for s in range(rows)], axis=1
            ) - update
            part_out[t + 1] = own
            copies = []
            for d in range(1, rows):
                copy = remote(
                    part_out.at[t + 1], part_in.at[t + 1, d], part_sems.at[0, t + 1, d],
                    part_sems.at[1, t + 1, d], "row", lax.rem(r + d, rows),
                )
                copy.start()
                copies.append(copy)
            pending += copies
            for j in range(rows_dev):
                acc[j] += lax.dot_general(
                    sent, factor[t][j], NT, preferred_element_type=jnp.float32
                )
        else:
            for j in range(rows_dev):
                total = acc[j] + lax.dot_general(
                    sent, factor[t][j], NT, preferred_element_type=jnp.float32
                )
                for s in range(rows):
                    tail_out[s, j] = total[:, s * width:(s + 1) * width]

    tails = []
    for d in range(1, rows):
        peer = lax.rem(r + d, rows)
        copy = remote(
            tail_out.at[peer], tail_in.at[d], tail_sems.at[0, d], tail_sems.at[1, d], "row", peer
        )
        copy.start()
        tails.append(copy)
    pending += tails
    for copy in tails:
        copy.wait_recv()
    for j in range(rows_dev):
        total = tail_out[r, j]
        for d in range(1, rows):
            total = total + tail_in[d, j]
        value = rhs[:, j, :] - total
        for t in range(sections):
            value = jnp.where(slots[t] == c * rows_dev + j, stored[t], value)
        out[:, j, :] = value
    for copy in pending:
        copy.wait_send()


def per_device(rows, cols, factor, diag_inverse, right_side, tile_order, live_segments):
    sections, width, tile = diag_inverse.shape
    rhs_count, rows_dev, _ = right_side.shape
    panel = jnp.transpose(factor, (1, 0, 2)).reshape(sections, rows_dev, tile, width)
    vmem = pl.BlockSpec(memory_space=pltpu.VMEM)
    smem = pl.BlockSpec(memory_space=pltpu.SMEM)
    hbm = pl.BlockSpec(memory_space=pl.ANY)
    f32, bf16 = jnp.float32, jnp.bfloat16
    return pl.pallas_call(
        functools.partial(kernel, rows, cols),
        out_shape=jax.ShapeDtypeStruct(right_side.shape, f32),
        in_specs=[hbm, hbm, vmem, smem, smem],
        out_specs=vmem,
        scratch_shapes=[
            [pltpu.VMEM((rows_dev, tile, width), bf16)] * sections,
            pltpu.VMEM((sections, width, tile), bf16),
            pltpu.VMEM((rows, rhs_count, width), f32),
            pltpu.VMEM((sections, rhs_count, tile), f32),
            pltpu.VMEM((sections, rows, rhs_count, tile), f32),
            [pltpu.VMEM((cols, rhs_count, width), bf16)] * sections,
            pltpu.VMEM((sections, rhs_count, width), f32),
            pltpu.VMEM((rows_dev, rhs_count, tile), f32),
            pltpu.VMEM((rows, rows_dev, rhs_count, width), f32),
            pltpu.VMEM((rows, rows_dev, rhs_count, width), f32),
            pltpu.SemaphoreType.DMA((sections,)),
            pltpu.SemaphoreType.DMA((sections,)),
            pltpu.SemaphoreType.DMA((2, rows)),
            pltpu.SemaphoreType.DMA((2, sections, rows)),
            pltpu.SemaphoreType.DMA((2, sections, cols)),
            pltpu.SemaphoreType.DMA((2, rows)),
        ],
        compiler_params=pltpu.CompilerParams(
            collective_id=0, has_side_effects=True, vmem_limit_bytes=48 * 2**20
        ),
    )(panel, diag_inverse, right_side, tile_order, live_segments)


def solution(mesh):
    return jax.shard_map(
        functools.partial(per_device, mesh.shape["row"], mesh.shape["col"]),
        mesh=mesh,
        in_specs=(P("col", None, "row"), P(None, "row", None), P(None, "col", "row"), P(), P()),
        out_specs=P(None, "col", "row"),
        check_vma=False,
    )
```

time: 293 us -> 72.2 us (0.25)
  waiting for transfers between devices: 178 us -> 0 us
  Pallas kernels: 0 us -> 67.5 us
  blocking collectives: 60.6 us -> 0 us
  between operations: 26 us -> 0.01 us
  matrix products: 18.2 us -> 0 us
  other arithmetic: 4.76 us -> 0 us
    psum x5 -> x0, waiting for transfers between devices: 159 us -> none  [per_device(): remaining = lax.psum(placed - part_tile, 'row')]
    pallas_call x0 -> x1, Pallas kernels: none -> 67.5 us  [per_device(): pl.pallas_call(functools.partial(kernel, rows, cols), out_shape=jax.Shape...]
    psum x5 -> x0, blocking collectives: 60.6 us -> none  [spread(): return lax.psum(block, axis)]
    reduce_scatter x1 -> x0, waiting for transfers between devices: 18.8 us -> none  [per_device(): lax.psum_scatter(shaped, 'row', scatter_dimension=2, tiled=True)]
    dot_general x10 -> x0, matrix products: 18.2 us -> none  [the longest x5 11.2 us: per_device(): lax.dot_general(sent_block, panel_rows, (((1,), (1,)), ((), ())), preferr...]
    unnamed x9, local copies, waits for them, and re-layouts: 1.49 us -> 4.52 us
  transfers between devices with their start and end apart: 6 -> 0, of which waited for: 6 -> 0; matrix products, arithmetic and copies ran while one was open for 0% -> 0% of each run, Pallas kernels for 0% -> 0%
where the time goes in v1:
time: 72.2 us; the launch traced here: 72 us
  Pallas kernels  67.5 us (93%)
  local copies, waits for them, and re-layouts  4.52 us (6%)
    pallas_call x1, Pallas kernels, per_device(): pl.pallas_call(functools.partial(kernel, rows, cols), out_shape=jax.Shape...  67.5 us
    unnamed x9, local copies, waits for them, and re-layouts  4.52 us

profile of v1, /device:TPU:0, one launch (start us, length us, event | category | flops | bytes accessed | tf_op | source)
XLA Modules:
  0.0 72.0 jit_solution(1810356289570610533)
XLA Ops:
  0.0 0.0 copy-start
  0.0 1.7 %copy-done = bf16[5,256,1024]{2,1,0:T(8,128)(2,1)S(1)} copy-done((bf16[5,256,1024]{2,1,0:T(8,128)(2,1)S(1)}, bf16[5,256,1024]{2,1,0:T(8,128)(2,1)}, u32[]{:S(2)}) %copy-start) | copy-done | bytes 2621464
  1.7 0.0 copy-start.1
  1.7 0.8 %copy-done.1 = f32[16,4,256]{2,1,0:T(4,128)S(1)} copy-done((f32[16,4,256]{2,1,0:T(4,128)S(1)}, f32[16,4,256]{2,1,0:T(4,128)}, u32[]{:S(2)}) %copy-start.1) | copy-done | bytes 65560
  2.6 0.0 copy-start.2
  2.6 0.7 copy-done.2
  3.2 0.0 copy-start.3
  3.2 0.7 copy-done.3
  3.9 67.5 %shard_map.55 = f32[16,4,256]{2,1,0:T(4,128)S(1)} custom-call(bf16[5,4,1024,256]{3,2,1,0:T(8,128)(2,1)} %bitcast.3, bf16[5,256,1024]{2,1,0:T(8,128)(2,1)S(1)} %copy-done, f32[16,4,256]{2,1,0:T(4,128)S(1)} %copy-done.1, s32[32]{0:T(128)S(1)} %copy-done.2, s32[16]{0:T(128)S(1)} %copy-done.3), custom_call_target="tpu_custom_call" | custom-call | tf_op jit(solution)/shard_map/pallas_call | solution.py:182
  71.4 0.6 copy.7
Async XLA Ops:
  0.0 1.7 %copy-start = (bf16[5,256,1024]{2,1,0:T(8,128)(2,1)S(1)}, bf16[5,256,1024]{2,1,0:T(8,128)(2,1)}, u32[]{:S(2)}) copy-start(bf16[5,256,1024]{2,1,0:T(8,128)(2,1)} %inverse_hbm.1) | copy-start | bytes 7864324
  1.7 0.8 %copy-start.1 = (f32[16,4,256]{2,1,0:T(4,128)S(1)}, f32[16,4,256]{2,1,0:T(4,128)}, u32[]{:S(2)}) copy-start(f32[16,4,256]{2,1,0:T(4,128)} %rhs.1) | copy-start | bytes 196612
  2.6 0.7 copy-start.2
  3.2 0.7 copy-start.3

commit v2 on v1

--- a/solution.py
+++ b/solution.py
@@ -7,7 +7,23 @@
 from jax.sharding import PartitionSpec as P
 
 MESH = pl.DeviceIdType.MESH
+SPARE = 128
 NT = (((1,), (1,)), ((), ()))
+
+
+def encode(value, spare):
+    peak = jnp.max(jnp.abs(value), axis=1, keepdims=True)
+    power = jnp.ceil(jnp.log2(jnp.maximum(peak, 1e-30)))
+    coded = jnp.floor(value * jnp.exp2(14.0 - power) + 0.5)
+    powers = jnp.broadcast_to(power, (value.shape[0], spare))
+    both = jnp.concatenate([coded, powers], axis=1)
+    return both.astype(jnp.int32).astype(jnp.int16)
+
+
+def decode(coded, count):
+    numbers = coded.astype(jnp.int32).astype(jnp.float32)
+    scale = jnp.exp2(numbers[:, count:count + 1] - 14.0)
+    return numbers[:, :count] * scale
 
 
 def remote(src, dst, send_sem, recv_sem, axis, peer):
@@ -18,15 +34,23 @@
 
 
 def kernel(
-    rows, cols, factor_hbm, inverse_hbm, rhs, order, live, out,
-    factor, inverse, first, part_out, part_in, sent_all, stored, acc, tail_out, tail_in,
-    factor_sem, inverse_sem, first_sems, part_sems, sent_sems, tail_sems,
+    rows, cols, factor_hbm, inverse_hbm, rhs_hbm, order_hbm, live_hbm, out,
+    factor, inverse, first, part_out, part_in, sent_all, stored, acc, tail_own, tail_out, tail_in,
+    rhs, order, live,
+    factor_sem, inverse_sem, first_sems, part_sems, sent_sems, tail_sems, small_sem,
 ):
     sections = len(factor)
     rows_dev, tile, width = factor[0].shape
     rhs_count = rhs.shape[0]
     r, c = lax.axis_index("row"), lax.axis_index("col")
 
+    small = (
+        pltpu.make_async_copy(rhs_hbm, rhs, small_sem.at[0]),
+        pltpu.make_async_copy(order_hbm, order, small_sem.at[1]),
+        pltpu.make_async_copy(live_hbm, live, small_sem.at[2]),
+    )
+    for copy in small:
+        copy.start()
     loads = []
     for u in range(sections):
         pair = (
@@ -44,6 +68,8 @@
                 barrier, inc=1, device_id={axis: lax.rem(me + d, count)}, device_id_type=MESH
             )
 
+    for copy in small:
+        copy.wait()
     slots = [order[u] for u in range(sections)]
     roots = [lax.div(s, rows_dev) for s in slots]
     locals_ = [lax.rem(s, rows_dev) for s in slots]
@@ -85,7 +111,7 @@
         else:
             remaining = own
             for d in range(1, rows):
-                remaining = remaining + part_in[t, d]
+                remaining = remaining + decode(part_in[t, d], tile)
             kept = remaining[:, :width]
             for s in range(1, rows):
                 kept = jnp.where(r == s, remaining[:, s * width:(s + 1) * width], kept)
@@ -126,7 +152,7 @@
             own = jnp.concatenate(
                 [jnp.where(r == s, mine, 0.0) for s in range(rows)], axis=1
             ) - update
-            part_out[t + 1] = own
+            part_out[t + 1] = encode(own, SPARE)
             copies = []
             for d in range(1, rows):
                 copy = remote(
@@ -145,8 +171,12 @@
                 total = acc[j] + lax.dot_general(
                     sent, factor[t][j], NT, preferred_element_type=jnp.float32
                 )
+                mine = total[:, :width]
+                for s in range(1, rows):
+                    mine = jnp.where(r == s, total[:, s * width:(s + 1) * width], mine)
+                tail_own[j] = mine
                 for s in range(rows):
-                    tail_out[s, j] = total[:, s * width:(s + 1) * width]
+                    tail_out[s, j] = encode(total[:, s * width:(s + 1) * width], SPARE)
 
     tails = []
     for d in range(1, rows):
@@ -160,9 +190,9 @@
     for copy in tails:
         copy.wait_recv()
     for j in range(rows_dev):
-        total = tail_out[r, j]
+        total = tail_own[j]
         for d in range(1, rows):
-            total = total + tail_in[d, j]
+            total = total + decode(tail_in[d, j], width)
         value = rhs[:, j, :] - total
         for t in range(sections):
             value = jnp.where(slots[t] == c * rows_dev + j, stored[t], value)
@@ -176,34 +206,38 @@
     rhs_count, rows_dev, _ = right_side.shape
     panel = jnp.transpose(factor, (1, 0, 2)).reshape(sections, rows_dev, tile, width)
     vmem = pl.BlockSpec(memory_space=pltpu.VMEM)
-    smem = pl.BlockSpec(memory_space=pltpu.SMEM)
     hbm = pl.BlockSpec(memory_space=pl.ANY)
-    f32, bf16 = jnp.float32, jnp.bfloat16
+    f32, bf16, i16 = jnp.float32, jnp.bfloat16, jnp.int16
     return pl.pallas_call(
         functools.partial(kernel, rows, cols),
         out_shape=jax.ShapeDtypeStruct(right_side.shape, f32),
-        in_specs=[hbm, hbm, vmem, smem, smem],
+        in_specs=[hbm] * 5,
         out_specs=vmem,
         scratch_shapes=[
             [pltpu.VMEM((rows_dev, tile, width), bf16)] * sections,
             pltpu.VMEM((sections, width, tile), bf16),
             pltpu.VMEM((rows, rhs_count, width), f32),
-            pltpu.VMEM((sections, rhs_count, tile), f32),
-            pltpu.VMEM((sections, rows, rhs_count, tile), f32),
+            pltpu.VMEM((sections, rhs_count, tile + SPARE), i16),
+            pltpu.VMEM((sections, rows, rhs_count, tile + SPARE), i16),
             [pltpu.VMEM((cols, rhs_count, width), bf16)] * sections,
             pltpu.VMEM((sections, rhs_count, width), f32),
             pltpu.VMEM((rows_dev, rhs_count, tile), f32),
-            pltpu.VMEM((rows, rows_dev, rhs_count, width), f32),
-            pltpu.VMEM((rows, rows_dev, rhs_count, width), f32),
+            pltpu.VMEM((rows_dev, rhs_count, width), f32),
+            pltpu.VMEM((rows, rows_dev, rhs_count, width + SPARE), i16),
+            pltpu.VMEM((rows, rows_dev, rhs_count, width + SPARE), i16),
+            pltpu.VMEM(right_side.shape, f32),
+            pltpu.SMEM(tile_order.shape, jnp.int32),
+            pltpu.SMEM(live_segments.shape, jnp.int32),
             pltpu.SemaphoreType.DMA((sections,)),
             pltpu.SemaphoreType.DMA((sections,)),
             pltpu.SemaphoreType.DMA((2, rows)),
             pltpu.SemaphoreType.DMA((2, sections, rows)),
             pltpu.SemaphoreType.DMA((2, sections, cols)),
             pltpu.SemaphoreType.DMA((2, rows)),
+            pltpu.SemaphoreType.DMA((3,)),
         ],
         compiler_params=pltpu.CompilerParams(
-            collective_id=0, has_side_effects=True, vmem_limit_bytes=48 * 2**20
+            collective_id=0, has_side_effects=True, vmem_limit_bytes=67043328
         ),
     )(panel, diag_inverse, right_side, tile_order, live_segments)
 

time: 72.2 us -> 60.8 us (0.84)
  Pallas kernels: 67.5 us -> 59.2 us
  local copies, waits for them, and re-layouts: 4.52 us -> 1.47 us
    pallas_call x1, Pallas kernels: 67.5 us -> 59.2 us  [per_device(): pl.pallas_call(functools.partial(kernel, rows, cols), out_shape=jax.Shape...]
    unnamed x9 -> x1, local copies, waits for them, and re-layouts: 4.52 us -> 1.47 us
where the time goes in v2:
time: 60.8 us; the launch traced here: 60.7 us
  Pallas kernels  59.2 us (97%)
  local copies, waits for them, and re-layouts  1.47 us (2%)
    pallas_call x1, Pallas kernels, per_device(): pl.pallas_call(functools.partial(kernel, rows, cols), out_shape=jax.Shape...  59.2 us
    unnamed x1, local copies, waits for them, and re-layouts  1.47 us

profile of v2, /device:TPU:0, one launch (start us, length us, event | category | flops | bytes accessed | tf_op | source)
XLA Modules:
  0.0 60.7 jit_solution(4201737617463930082)
XLA Ops:
  0.0 59.2 %shard_map.55 = f32[16,4,256]{2,1,0:T(4,128)} custom-call(bf16[5,4,1024,256]{3,2,1,0:T(8,128)(2,1)} %bitcast.3, bf16[5,256,1024]{2,1,0:T(8,128)(2,1)} %inverse_hbm.1, f32[16,4,256]{2,1,0:T(4,128)} %rhs_hbm.1, s32[32]{0:T(128)} %order_hbm.1, s32[16]{0:T(128)} %live_hbm.1), custom_call_target="tpu_custom_call" | custom-call | tf_op jit(solution)/shard_map/pallas_call | solution.py:211
  59.2 1.5 %copy.7 = f32[16,4,256]{2,1,0:T(4,128)} copy(f32[16,4,256]{2,1,0:T(4,128)} %shard_map.55) | data formatting | bytes 131072
